TPU v7x, 128 devices: a whole 4x4x4 slice. The times are simulated.
128 devices in a mesh: fsdp: 8 (over x, y_lo), tensor: 16 (over z, y_hi, core).
Axes of the slice: x: 4, y: 4 (y_hi: 2, y_lo: 2; y = y_hi * 2 + y_lo), z: 4, core: 2. Of those that a mesh axis runs over, the one named last changes fastest.
Arguments:
- modality: int32 [8192], P('fsdp'), may hold values from 0 to 2, as said below
- out_grad: bfloat16 [8192, 4096], P('fsdp', 'tensor'), may hold values from -6 to 6
- gate_pre: bfloat16 [8192, 11008], P('fsdp', 'tensor'), may hold values from -6 to 6
- up_pre: bfloat16 [8192, 11008], P('fsdp', 'tensor'), may hold values from -6 to 6
- down_weight: bfloat16 [3, 11008, 4096], P(None, 'tensor', 'fsdp'), may hold values from -0.0546875 to 0.0546875
Outputs:
- down_grad: float32 [3, 11008, 4096], P(None, 'tensor', 'fsdp')
- gate_grad: bfloat16 [8192, 11008], P('fsdp', 'tensor')
- up_grad: bfloat16 [8192, 11008], P('fsdp', 'tensor')
Inputs may be any that keep to these rules, and one draw needn't show every extreme that they name: `modality`: the 1024 tokens of every index of fsdp hold each of the three modalities at least once.
All inputs are finite; a program needn't handle non-finite values.
Results may differ from a plain program's by a relative error of at most 0.012.
Values may be sent and summed in bfloat16 or wider, within the bound.
No kernel may reach another device: no remote copies, remote signals or barrier semaphores. Data moves between devices by JAX's collectives and lax.ppermute only.
A program may use at most 256 MiB of HBM per device.

v0:
```python
import math
import jax
import jax.numpy as jnp
from jax import lax
from jax.sharding import Mesh
from jax.sharding import PartitionSpec as P

FSDP = ("fsdp_0", "fsdp_1")


def sent_to_all(shard, axis):
    peers = lax.axis_size(axis)
    return lax.all_to_all(
        jnp.broadcast_to(shard[None], (peers, *shard.shape)), axis, 0, 0, tiled=True
    )


def taken_together(shard, axis):
    return sent_to_all(shard, axis).sum(axis=0)


def gather_axes(shard, axes, dim):
    for axis in reversed(axes):
        shard = lax.all_gather(shard, axis, axis=dim, tiled=True)
    return shard


def sum_by_axis(shard, axes, dim):
    for axis in axes:
        shard = lax.psum_scatter(shard, axis, scatter_dimension=dim, tiled=True)
    return shard


def kind_table(kind_ids):
    labels = jnp.arange(3, dtype=jnp.int32)
    return (kind_ids[:, None] == labels[None, :]).astype(jnp.float32)


def shards(modality, out_grad, gate_pre, up_pre, down_weight):
    tok_rows = modality.shape[0]
    groups = lax.axis_size(FSDP)
    local_onehot = kind_table(modality)
    counts = taken_together(jnp.sum(local_onehot, axis=0), FSDP)
    factor = tok_rows * groups / (3.0 * counts)
    token_scale = jnp.sum(local_onehot * factor[None, :], axis=1)
    scaled_part = (out_grad.astype(jnp.float32) * token_scale[:, None]).astype(jnp.bfloat16)
    scaled = lax.all_gather(scaled_part, "tensor", axis=1, tiled=True)
    gate_val = gate_pre.astype(jnp.float32)
    up_val = up_pre.astype(jnp.float32)
    sigmoid_g = jax.nn.sigmoid(gate_val)
    active = gate_val * sigmoid_g
    hidden = (active * up_val).astype(jnp.bfloat16)
    hid_cols = hidden.shape[1]
    width_all = scaled.shape[1]
    block_rows = math.gcd(tok_rows, 128)
    block_count = tok_rows // block_rows + 2
    capacity = block_count * block_rows
    int_onehot = local_onehot.astype(jnp.int32)
    slot_rank = jnp.sum((jnp.cumsum(int_onehot, axis=0) - int_onehot) * int_onehot, axis=1)
    used_rows = jnp.sum(int_onehot, axis=0)
    padded = (used_rows + block_rows - 1) // block_rows * block_rows
    second = padded[0]
    third_start = padded[0] + padded[1]
    starts = jnp.stack([jnp.zeros((), jnp.int32), second, third_start])
    slot_index = jnp.sum(int_onehot * starts[None, :], axis=1) + slot_rank
    block_first = jnp.arange(block_count, dtype=jnp.int32) * block_rows
    block_kind = (block_first >= second).astype(jnp.int32) + (block_first >= third_start).astype(
        jnp.int32
    )
    packed_scaled = jnp.zeros((capacity, width_all), jnp.bfloat16).at[slot_index].set(scaled)
    packed_hidden = jnp.zeros((capacity, hid_cols), jnp.bfloat16).at[slot_index].set(hidden)
    weight_piece = gather_axes(down_weight, FSDP, 2)
    columns_here = weight_piece.shape[2]
    columns = packed_scaled
    columns = columns.reshape(block_count, block_rows, columns_here)
    chosen = jnp.take(weight_piece, block_kind, axis=0)
    product = jnp.einsum("bkw,bfw->bkf", columns, chosen, preferred_element_type=jnp.float32)
    folded = product.reshape(capacity, hid_cols)
    d_hidden = folded[slot_index]
    up_grad = (d_hidden * active).astype(jnp.bfloat16)
    slope = sigmoid_g * (1.0 + gate_val * (1.0 - sigmoid_g))
    gate_grad = (d_hidden * up_val * slope).astype(jnp.bfloat16)

    def kind_product(kind_id):
        first_block = starts[kind_id] // block_rows
        last_block = first_block + padded[kind_id] // block_rows

        def add_block(block_index, running):
            rows_hidden = lax.dynamic_slice_in_dim(
                packed_hidden, block_index * block_rows, block_rows, 0
            )
            rows_scaled = lax.dynamic_slice_in_dim(
                packed_scaled, block_index * block_rows, block_rows, 0
            )
            return running + lax.dot_general(
                rows_hidden,
                rows_scaled,
                (((0,), (0,)), ((), ())),
                preferred_element_type=jnp.float32,
            )

        return lax.fori_loop(
            first_block, last_block, add_block, jnp.zeros((hid_cols, width_all), jnp.float32)
        )

    partial_sum = jnp.stack([kind_product(kind_id) for kind_id in range(3)])
    down_grad = sum_by_axis(partial_sum.astype(jnp.bfloat16), FSDP, 2).astype(jnp.float32)
    return (down_grad, gate_grad, up_grad)


def solution(mesh):
    torus = Mesh(mesh.devices.reshape(4, 2, mesh.shape["tensor"]), ("fsdp_0", "fsdp_1", "tensor"))
    in_specs = (
        P(FSDP),
        P(FSDP, "tensor"),
        P(FSDP, "tensor"),
        P(FSDP, "tensor"),
        P(None, "tensor", FSDP),
    )
    out_specs = (P(None, "tensor", FSDP), P(FSDP, "tensor"), P(FSDP, "tensor"))
    return jax.shard_map(
        shards, mesh=torus, in_specs=in_specs, out_specs=out_specs, check_vma=False
    )
```

profile of v0, /device:TPU:1, one launch (start us, length us, event | category | flops | bytes accessed | tf_op | source)
XLA Modules:
  0.0 537.5 jit_solution(230502349124138979)
XLA Ops:
  23.1 49.2 %all-gather.6.cloned.1.call-done = bf16[3,688,1024]{2,1,0:T(8,128)(2,1)} async-done(((bf16[3,688,512]{2,1,0:T(8,128)(2,1)}), bf16[3,688,1024]{2,1,0:T(8,128)(2,1)}) %all-gather.6.cloned.1.call-update) | async-done | bytes 4227088 | tf_op jit(solution)/shard_map/all_gather | solution.py:24
  94.8 58.6 %all-gather.4.cloned.1.call-done = bf16[1024,4096]{1,0:T(8,128)(2,1)} async-done(((bf16[1024,256]{1,0:T(8,128)(2,1)}), bf16[1024,4096]{1,0:T(8,128)(2,1)}) %all-gather.4.cloned.1.call-update) | async-done | bytes 8388624 | tf_op jit(solution)/shard_map/all_gather | solution.py:47
  153.4 19.3 %scatter_custom_fusion.1 = bf16[1280,4096]{1,0:T(8,128)(2,1)} fusion(s32[1024]{0:T(1024)S(1)} %bitcast.35, bf16[1024,4096]{1,0:T(8,128)(2,1)} %all-gather.4.cloned.1.call-done, bf16[]{:T(256)} %constant.116.clone.1), kind=kCustom, calls=%fused_computation.30 | custom fusion | bytes 10486272 | tf_op jit(solution)/shard_map/scatter | solution.py:70
  178.4 31.6 %while.30 = (s32[]{:T(128)}, f32[688,4096]{1,0:T(8,128)}, s32[]{:T(128)}, bf16[1280,688]{1,0:T(8,128)(2,1)}, bf16[1280,4096]{1,0:T(8,128)(2,1)}, /*index=5*/s32[]{:T(128)}, s32[]{:T(128)}, s32[]{:T(128)}, s32[]{:T(128)}) while((s32[]{:T(128)}, f32[688,4096]{1,0:T(8,128)}, s32[]{:T(128)}, bf16[1280,688]{1,0:T(8,128)(2,1)}, ...), condition=%wide.region_11.12_spmd, body=%wide.region_10.11_spmd.sunk | while | flops 724238336 | bytes 23790732 | solution.py:102
  178.4 10.5 %convolution_add_fusion.6 = f32[688,4096]{1,0:T(8,128)} fusion(f32[688,4096]{1,0:T(8,128)} %get-tuple-element.306, bf16[1280,4096]{1,0:T(8,128)(2,1)} %get-tuple-element.318, s32[]{:T(128)S(6)} %select_n.91, bf16[1280,688]{1,0:T(8,128)(2,1)} %get-tuple-element.317), kind=kOutput, calls=%fused_computation.6.clone.1 | convolution fusion | flops 724238336 | bytes 23790592 | tf_op jit(solution)/shard_map/while/body/dot_general | solution.py:95
  188.9 10.5 %convolution_add_fusion.6 = f32[688,4096]{1,0:T(8,128)} fusion(f32[688,4096]{1,0:T(8,128)} %get-tuple-element.306, bf16[1280,4096]{1,0:T(8,128)(2,1)} %get-tuple-element.318, s32[]{:T(128)S(6)} %select_n.91, bf16[1280,688]{1,0:T(8,128)(2,1)} %get-tuple-element.317), kind=kOutput, calls=%fused_computation.6.clone.1 | convolution fusion | flops 724238336 | bytes 23790592 | tf_op jit(solution)/shard_map/while/body/dot_general | solution.py:95
  199.4 10.6 %convolution_add_fusion.6 = f32[688,4096]{1,0:T(8,128)} fusion(f32[688,4096]{1,0:T(8,128)} %get-tuple-element.306, bf16[1280,4096]{1,0:T(8,128)(2,1)} %get-tuple-element.318, s32[]{:T(128)S(6)} %select_n.91, bf16[1280,688]{1,0:T(8,128)(2,1)} %get-tuple-element.317), kind=kOutput, calls=%fused_computation.6.clone.1 | convolution fusion | flops 724238336 | bytes 23790592 | tf_op jit(solution)/shard_map/while/body/dot_general | solution.py:95
  223.2 20.8 %while.31 = (s32[]{:T(128)}, f32[688,4096]{1,0:T(8,128)}, s32[]{:T(128)}, bf16[1280,688]{1,0:T(8,128)(2,1)}, bf16[1280,4096]{1,0:T(8,128)(2,1)}, /*index=5*/s32[]{:T(128)}, s32[]{:T(128)}, s32[]{:T(128)}, s32[]{:T(128)}) while((s32[]{:T(128)}, f32[688,4096]{1,0:T(8,128)}, s32[]{:T(128)}, bf16[1280,688]{1,0:T(8,128)(2,1)}, ...), condition=%wide.region_13.14_spmd, body=%wide.region_12.13_spmd.sunk | while | flops 724238336 | bytes 23790732 | solution.py:102
  223.2 10.4 %convolution_add_fusion.7 = f32[688,4096]{1,0:T(8,128)} fusion(f32[688,4096]{1,0:T(8,128)} %get-tuple-element.279, bf16[1280,4096]{1,0:T(8,128)(2,1)} %get-tuple-element.291, s32[]{:T(128)S(6)} %select_n.92, bf16[1280,688]{1,0:T(8,128)(2,1)} %get-tuple-element.290), kind=kOutput, calls=%fused_computation.10.clone.1 | convolution fusion | flops 724238336 | bytes 23790592 | tf_op jit(solution)/shard_map/while/body/dot_general | solution.py:95
  233.6 10.4 %convolution_add_fusion.7 = f32[688,4096]{1,0:T(8,128)} fusion(f32[688,4096]{1,0:T(8,128)} %get-tuple-element.279, bf16[1280,4096]{1,0:T(8,128)(2,1)} %get-tuple-element.291, s32[]{:T(128)S(6)} %select_n.92, bf16[1280,688]{1,0:T(8,128)(2,1)} %get-tuple-element.290), kind=kOutput, calls=%fused_computation.10.clone.1 | convolution fusion | flops 724238336 | bytes 23790592 | tf_op jit(solution)/shard_map/while/body/dot_general | solution.py:95
  249.6 42.1 %while.32 = (s32[]{:T(128)}, f32[688,4096]{1,0:T(8,128)}, s32[]{:T(128)}, bf16[1280,688]{1,0:T(8,128)(2,1)}, bf16[1280,4096]{1,0:T(8,128)(2,1)}, /*index=5*/s32[]{:T(128)}, s32[]{:T(128)}, s32[]{:T(128)}, s32[]{:T(128)}) while((s32[]{:T(128)}, f32[688,4096]{1,0:T(8,128)}, s32[]{:T(128)}, bf16[1280,688]{1,0:T(8,128)(2,1)}, ...), condition=%wide.region_15.16_spmd, body=%wide.region_14.15_spmd.sunk | while | flops 724238336 | bytes 23790732 | solution.py:102
  249.6 10.6 %convolution_add_fusion.8 = f32[688,4096]{1,0:T(8,128)} fusion(f32[688,4096]{1,0:T(8,128)} %get-tuple-element.252, bf16[1280,4096]{1,0:T(8,128)(2,1)} %get-tuple-element.264, s32[]{:T(128)S(6)} %select_n.93, bf16[1280,688]{1,0:T(8,128)(2,1)} %get-tuple-element.263), kind=kOutput, calls=%fused_computation.14.clone.1 | convolution fusion | flops 724238336 | bytes 23790592 | tf_op jit(solution)/shard_map/while/body/dot_general | solution.py:95
  260.2 10.6 %convolution_add_fusion.8 = f32[688,4096]{1,0:T(8,128)} fusion(f32[688,4096]{1,0:T(8,128)} %get-tuple-element.252, bf16[1280,4096]{1,0:T(8,128)(2,1)} %get-tuple-element.264, s32[]{:T(128)S(6)} %select_n.93, bf16[1280,688]{1,0:T(8,128)(2,1)} %get-tuple-element.263), kind=kOutput, calls=%fused_computation.14.clone.1 | convolution fusion | flops 724238336 | bytes 23790592 | tf_op jit(solution)/shard_map/while/body/dot_general | solution.py:95
  270.8 10.5 %convolution_add_fusion.8 = f32[688,4096]{1,0:T(8,128)} fusion(f32[688,4096]{1,0:T(8,128)} %get-tuple-element.252, bf16[1280,4096]{1,0:T(8,128)(2,1)} %get-tuple-element.264, s32[]{:T(128)S(6)} %select_n.93, bf16[1280,688]{1,0:T(8,128)(2,1)} %get-tuple-element.263), kind=kOutput, calls=%fused_computation.14.clone.1 | convolution fusion | flops 724238336 | bytes 23790592 | tf_op jit(solution)/shard_map/while/body/dot_general | solution.py:95
  281.3 10.5 %convolution_add_fusion.8 = f32[688,4096]{1,0:T(8,128)} fusion(f32[688,4096]{1,0:T(8,128)} %get-tuple-element.252, bf16[1280,4096]{1,0:T(8,128)(2,1)} %get-tuple-element.264, s32[]{:T(128)S(6)} %select_n.93, bf16[1280,688]{1,0:T(8,128)(2,1)} %get-tuple-element.263), kind=kOutput, calls=%fused_computation.14.clone.1 | convolution fusion | flops 724238336 | bytes 23790592 | tf_op jit(solution)/shard_map/while/body/dot_general | solution.py:95
  291.8 8.3 %convert_bitcast_fusion = (bf16[1,688,4096]{2,1,0:T(8,128)(2,1)S(1)}, bf16[1,688,4096]{2,1,0:T(8,128)(2,1)S(1)}) fusion(f32[688,4096]{1,0:T(8,128)} %get-tuple-element.89, f32[688,4096]{1,0:T(8,128)} %get-tuple-element.88), kind=kLoop, calls=%fused_computation.27 | loop fusion | flops 5636096 | bytes 33816576 | tf_op jit(solution)/shard_map/stack | solution.py:106
  300.1 10.1 %pad_maximum_fusion = bf16[3,688,4096]{2,1,0:T(8,128)(2,1)} fusion(bf16[1,688,4096]{2,1,0:T(8,128)(2,1)S(1)} %get-tuple-element.144, bf16[1,688,4096]{2,1,0:T(8,128)(2,1)S(1)} %get-tuple-element.145, bf16[1,688,4096]{2,1,0:T(8,128)(2,1)} %convert_bitcast_fusion.2), kind=kLoop, calls=%fused_computation.26 | loop fusion | flops 16908288 | bytes 33816576 | tf_op jit(solution)/shard_map/stack | solution.py:106
  312.4 9.8 %fusion.39 = (bf16[3,688,1408]{2,1,0:T(8,128)(2,1)}, bf16[3,688,1408]{2,1,0:T(8,128)(2,1)}) fusion(bf16[3,688,4096]{2,1,0:T(8,128)(2,1)} %all-gather.8.cloned.1.call-done), kind=kLoop, calls=%fused_computation.85 | loop fusion | bytes 23248896 | tf_op jit(solution)/shard_map/jit(_take)/gather | solution.py:76
  322.1 14.4 %gather_fusion.1 = bf16[10,688,1408]{2,1,0:T(8,128)(2,1)} fusion(bf16[3,688,1408]{2,1,0:T(8,128)(2,1)} %get-tuple-element.137, s32[1024]{0:T(1024)S(1)} %pad_clamp_fusion), kind=kCustom, calls=%fused_computation.1 | custom fusion | bytes 38748200 | tf_op jit(solution)/shard_map/jit(_take)/gather | solution.py:76
  336.5 14.3 %gather_fusion.2 = bf16[10,688,1408]{2,1,0:T(8,128)(2,1)} fusion(bf16[3,688,1408]{2,1,0:T(8,128)(2,1)} %get-tuple-element.138, s32[1024]{0:T(1024)S(1)} %pad_clamp_fusion), kind=kCustom, calls=%fused_computation.2 | custom fusion | bytes 38748200 | tf_op jit(solution)/shard_map/jit(_take)/gather | solution.py:76
  356.1 11.0 %gather_fusion.3 = bf16[10,688,1280]{2,1,0:T(8,128)(2,1)} fusion(bf16[3,688,1280]{2,1,0:T(8,128)(2,1)} %mini-gather-slice.5, s32[1024]{0:T(1024)S(1)} %pad_clamp_fusion), kind=kCustom, calls=%fused_computation.3 | custom fusion | bytes 35225640 | tf_op jit(solution)/shard_map/jit(_take)/gather | solution.py:76
  367.1 100.5 %reduce-scatter.3.cloned.1.call-done = bf16[3,688,1024]{2,1,0:T(8,128)(2,1)} async-done(((bf16[3,688,4096]{2,1,0:T(8,128)(2,1)}), bf16[3,688,1024]{2,1,0:T(8,128)(2,1)}) %reduce-scatter.3.cloned.1.call-update) | async-done | bytes 4227088 | tf_op jit(solution)/shard_map/reduce_scatter | solution.py:30
  467.6 33.8 %fusion.9 = f32[10,128,688]{2,1,0:T(8,128)} fusion(bf16[10,128,4096]{2,1,0:T(8,128)(2,1)} %bitcast.31, bf16[10,688,1280]{2,1,0:T(8,128)(2,1)} %gather_fusion.3, bf16[10,688,1408]{2,1,0:T(8,128)(2,1)} %gather_fusion.2, bf16[10,688,1408]{2,1,0:T(8,128)(2,1)} %gather_fusion.1, pred[10]{0:T(512)(128)(4,1)S(1)} %compare_and_fusion), kind=kOutput, calls=%fused_computation.19 | convolution fusion | flops 7411466240 | bytes 70369288 | tf_op jit(solution)/shard_map/bkw,bfw->bkf/dot_general | solution.py:77
  501.4 8.1 %gather_fusion = f32[1024,688]{1,0:T(8,128)} fusion(f32[1280,688]{1,0:T(8,128)} %bitcast.30, s32[1024]{0:T(1024)S(1)} %copy-done.8), kind=kCustom, calls=%fused_computation | custom fusion | bytes 5640192 | tf_op jit(solution)/shard_map/gather | solution.py:79
  (66 shorter events, 82.6 us)
Async XLA Ops:
  7.2 65.2 %copy-start.5 = (s32[1024]{0:T(1024)S(1)}, s32[1024]{0:T(1024)}, u32[]{:S(2)}) copy-start(s32[1024]{0:T(1024)} %param.11) | copy-start | bytes 12292
  7.2 76.3 %copy-start.4 = (bf16[1024,688]{0,1:T(8,128)(2,1)S(1)}, bf16[1024,688]{0,1:T(8,128)(2,1)}, u32[]{:S(2)}) copy-start(bf16[1024,688]{0,1:T(8,128)(2,1)} %param.13) | copy-start | bytes 4227076
  7.2 65.1 %all-gather.6.cloned.1.call-start = ((), (), s32[]{:S(2)}) async-start(), calls=%async_computation.6 | async-start | bytes 6340608 | tf_op jit(solution)/shard_map/all_gather | solution.py:24
  9.3 10.8 %all-to-all-start = ((f32[8,1,3]{2,1,0:T(1,128)}), f32[8,1,3]{2,1,0:T(1,128)S(1)}, u32[]{:S(2)}, u32[]{:S(2)}) async-start(f32[8,1,3]{2,1,0:T(1,128)} %broadcast_in_dim.15), calls=%async_computation | async-start | bytes 8192 | tf_op jit(solution)/shard_map/all_to_all | solution.py:13
  15.2 138.2 %all-gather.4.cloned.1.call-start = ((), (), s32[]{:S(2)}) async-start(), calls=%async_computation.3 | async-start | bytes 8912896 | tf_op jit(solution)/shard_map/all_gather | solution.py:47
  23.1 289.3 %all-gather.8.cloned.1.call-start = ((), (), s32[]{:S(2)}) async-start(), calls=%async_computation.7 | async-start | bytes 21135360 | tf_op jit(solution)/shard_map/all_gather | solution.py:24
  72.4 395.2 %reduce-scatter.3.cloned.1.call-start = ((), (), s32[]{:S(2)}) async-start(), calls=%async_computation.4 | async-start | bytes 21135360 | tf_op jit(solution)/shard_map/reduce_scatter | solution.py:30
  84.1 88.6 %copy-start = (bf16[1024,688]{1,0:T(8,128)(2,1)}, bf16[1024,688]{1,0:T(8,128)(2,1)S(1)}, u32[]{:S(2)}) copy-start(bf16[1024,688]{1,0:T(8,128)(2,1)S(1)} %copy.28) | copy-start | bytes 4227076
  86.4 86.4 %copy-start.2 = (bf16[1024,688]{1,0:T(8,128)(2,1)}, bf16[1024,688]{1,0:T(8,128)(2,1)S(1)}, u32[]{:S(2)}) copy-start(bf16[1024,688]{1,0:T(8,128)(2,1)S(1)} %copy.29) | copy-start | bytes 4227076
  87.4 85.4 %copy-start.6 = (s32[1024,1]{0,1:T(1,128)}, s32[1024,1]{0,1:T(1,128)S(1)}, u32[]{:S(2)}) copy-start(s32[1024,1]{0,1:T(1,128)S(1)} %compare_select_fusion) | copy-start | bytes 12292
  310.1 1.6 copy-start.7
  310.2 216.6 %reduce-scatter.5.cloned.1.call-start = ((), (), s32[]{:S(2)}) async-start(), calls=%async_computation.5 | async-start | bytes 6340608 | tf_op jit(solution)/shard_map/reduce_scatter | solution.py:30
  467.6 33.8 %copy-start.8 = (s32[1024]{0:T(1024)S(1)}, s32[1024]{0:T(1024)}, u32[]{:S(2)}) copy-start(s32[1024]{0:T(1024)} %broadcast_clamp_fusion) | copy-start | bytes 12292
  501.4 8.1 %copy-start.1 = (bf16[1024,688]{1,0:T(8,128)(2,1)S(1)}, bf16[1024,688]{1,0:T(8,128)(2,1)}, u32[]{:S(2)}) copy-start(bf16[1024,688]{1,0:T(8,128)(2,1)} %copy-done) | copy-start | bytes 4227076
  501.4 8.1 %copy-start.3 = (bf16[1024,688]{1,0:T(8,128)(2,1)S(1)}, bf16[1024,688]{1,0:T(8,128)(2,1)}, u32[]{:S(2)}) copy-start(bf16[1024,688]{1,0:T(8,128)(2,1)} %copy-done.2) | copy-start | bytes 4227076
Sparse Core Ops, SparseCore 0:
  9.6 62.6 all-gather.5
  75.2 78.1 all-gather.3
  155.1 153.0 all-gather.7
  310.6 156.9 reduce-scatter.2
  469.8 56.8 reduce-scatter.4
where the time goes:
time: 539 us; the launch traced here: 537 us
  waiting for transfers between devices  221 us (41%)
  matrix products  128 us (24%)
  local copies, waits for them, and re-layouts  108 us (20%)
  other arithmetic  50.4 us (9%)
  between operations  23 us (4%)
  starting transfers between devices  6.31 us (1%)
    reduce_scatter x2, waiting for transfers between devices, sum_by_axis(): shard = lax.psum_scatter(shard, axis, scatter_dimension=dim, tiled=True)  108 us
    dot_general x9, matrix products, add_block(): lax.dot_general(rows_hidden, rows_scaled, (((0,), (0,)), ((), ())), prefe...  94.5 us
    all_gather x1, waiting for transfers between devices, shards(): scaled = lax.all_gather(scaled_part, 'tensor', axis=1, tiled=True)  58.6 us
    gather x5, local copies, waits for them, and re-layouts, shards(): chosen = jnp.take(weight_piece, block_kind, axis=0)  54.7 us
    all_gather x2, waiting for transfers between devices, gather_axes(): shard = lax.all_gather(shard, axis, axis=dim, tiled=True)  49.2 us
    dot_general x1, matrix products, shards(): jnp.einsum('bkw,bfw->bkf', columns, chosen, preferred_element_type=jnp.fl...  33.8 us
    another operation x3, other arithmetic, shards(): partial_sum = jnp.stack([kind_product(kind_id) for kind_id in range(3)])  26 us
    scatter x1, local copies, waits for them, and re-layouts, shards(): jnp.zeros((capacity, width_all), jnp.bfloat16).at[slot_index].set(scaled)  19.3 us
  transfers between devices with their start and end apart: 6, of which 5 were waited for; matrix products, arithmetic and copies ran while one was open for 53% of the time, Pallas kernels for 0%

commit v1 on v0

--- a/solution.py
+++ b/solution.py
@@ -1,3 +1,4 @@
+import functools
 import math
 import jax
 import jax.numpy as jnp
@@ -6,6 +7,21 @@
 from jax.sharding import PartitionSpec as P
 
 FSDP = ("fsdp_0", "fsdp_1")
+
+
+def records_prepare(raw, d_out):
+    return jnp.concatenate(
+        lax.all_to_all(
+            jnp.stack([raw] * lax.axis_size("tensor")),
+            split_axis=0,
+            axis_name="tensor",
+            concat_axis=0,
+        ),
+        axis=d_out,
+    )
+
+
+begin_column = functools.partial(records_prepare, d_out=1)
 
 
 def sent_to_all(shard, axis):
@@ -44,7 +60,7 @@
     factor = tok_rows * groups / (3.0 * counts)
     token_scale = jnp.sum(local_onehot * factor[None, :], axis=1)
     scaled_part = (out_grad.astype(jnp.float32) * token_scale[:, None]).astype(jnp.bfloat16)
-    scaled = lax.all_gather(scaled_part, "tensor", axis=1, tiled=True)
+    scaled = begin_column(scaled_part)
     gate_val = gate_pre.astype(jnp.float32)
     up_val = up_pre.astype(jnp.float32)
     sigmoid_g = jax.nn.sigmoid(gate_val)

time: 539 us -> 602 us (1.12)
  local copies, waits for them, and re-layouts: 108 us -> 136 us
  waiting for transfers between devices: 221 us -> 249 us
  starting transfers between devices: 6.31 us -> 13.4 us
    all_to_all x0 -> x1, waiting for transfers between devices: none -> 73.1 us  [records_prepare(): lax.all_to_all(jnp.stack([raw] * lax.axis_size('tensor')), split_axis=0,...]
    all_gather x1 -> x0, waiting for transfers between devices: 58.6 us -> none  [shards(): scaled = lax.all_gather(scaled_part, 'tensor', axis=1, tiled=True)]
    all_gather x2, waiting for transfers between devices: 49.2 us -> 64.4 us  [gather_axes(): shard = lax.all_gather(shard, axis, axis=dim, tiled=True)]
    all_to_all x0 -> x1, local copies, waits for them, and re-layouts: none -> 12.3 us  [records_prepare(): lax.all_to_all(jnp.stack([raw] * lax.axis_size('tensor')), split_axis=0,...]
    reshape x0 -> x1, local copies, waits for them, and re-layouts: none -> 11.3 us  [records_prepare(): jnp.concatenate(lax.all_to_all(jnp.stack([raw] * lax.axis_size('tensor'))...]
    all_to_all x0 -> x1, starting transfers between devices: none -> 9 us  [records_prepare(): lax.all_to_all(jnp.stack([raw] * lax.axis_size('tensor')), split_axis=0,...]
    another operation x3 -> x4, local copies, waits for them, and re-layouts: 16.8 us -> 22 us
  transfers between devices with their start and end apart: 6 -> 6, of which waited for: 5 -> 5; matrix products, arithmetic and copies ran while one was open for 53% -> 52% of each run, Pallas kernels for 0% -> 0%
where the time goes in v1:
time: 602 us; the launch traced here: 600 us
  waiting for transfers between devices  249 us (41%)
  local copies, waits for them, and re-layouts  136 us (23%)
  matrix products  128 us (21%)
  other arithmetic  49.7 us (8%)
  between operations  23.2 us (4%)
  starting transfers between devices  13.4 us (2%)
    reduce_scatter x2, waiting for transfers between devices, sum_by_axis(): shard = lax.psum_scatter(shard, axis, scatter_dimension=dim, tiled=True)  106 us
    dot_general x9, matrix products, add_block(): lax.dot_general(rows_hidden, rows_scaled, (((0,), (0,)), ((), ())), prefe...  94.3 us
    all_to_all x1, waiting for transfers between devices, records_prepare(): lax.all_to_all(jnp.stack([raw] * lax.axis_size('tensor')), split_axis=0,...  73.1 us
    all_gather x2, waiting for transfers between devices, gather_axes(): shard = lax.all_gather(shard, axis, axis=dim, tiled=True)  64.4 us
    gather x5, local copies, waits for them, and re-layouts, shards(): chosen = jnp.take(weight_piece, block_kind, axis=0)  54.1 us
    dot_general x1, matrix products, shards(): jnp.einsum('bkw,bfw->bkf', columns, chosen, preferred_element_type=jnp.fl...  33.8 us
    another operation x3, other arithmetic, shards(): partial_sum = jnp.stack([kind_product(kind_id) for kind_id in range(3)])  25.9 us
    scatter x1, local copies, waits for them, and re-layouts, shards(): jnp.zeros((capacity, width_all), jnp.bfloat16).at[slot_index].set(scaled)  18.7 us
  transfers between devices with their start and end apart: 6, of which 5 were waited for; matrix products, arithmetic and copies ran while one was open for 52% of the time, Pallas kernels for 0%

profile of v1, /device:TPU:1, one launch (start us, length us, event | category | flops | bytes accessed | tf_op | source)
XLA Modules:
  0.0 599.8 jit_solution(13562110322689542036)
XLA Ops:
  7.9 64.4 %all-gather.3.cloned.1.call-done = bf16[3,688,1024]{2,1,0:T(8,128)(2,1)} async-done(((bf16[3,688,512]{2,1,0:T(8,128)(2,1)}), bf16[3,688,1024]{2,1,0:T(8,128)(2,1)}) %all-gather.3.cloned.1.call-update) | async-done | bytes 4227088 | tf_op jit(solution)/shard_map/all_gather | solution.py:40
  121.8 73.1 %all-to-all-done.1 = bf16[16,1024,256]{2,1,0:T(8,128)(2,1)} async-done(((bf16[16,1024,256]{2,1,0:T(8,128)(2,1)}), bf16[16,1024,256]{2,1,0:T(8,128)(2,1)}, u32[]{:S(2)}, u32[]{:S(2)}) %all-to-all-start.1) | async-done | bytes 8388640 | tf_op jit(solution)/shard_map/all_to_all | solution.py:14
  194.8 12.3 %copy.53 = bf16[16,1024,256]{1,2,0:T(8,128)(2,1)} copy(bf16[16,1024,256]{2,1,0:T(8,128)(2,1)} %all-to-all-done.1) | data formatting | bytes 16777216 | tf_op jit(solution)/shard_map/all_to_all | solution.py:14
  207.1 11.3 %copy.54 = bf16[1024,4096]{1,0:T(8,128)(2,1)} copy(bf16[1024,4096]{0,1:T(8,128)(2,1)} %bitcast.35) | data formatting | bytes 16777216 | tf_op jit(solution)/shard_map/reshape | solution.py:13
  218.4 18.7 %scatter_custom_fusion.1 = bf16[1280,4096]{1,0:T(8,128)(2,1)} fusion(s32[1024]{0:T(1024)S(1)} %bitcast.39, bf16[1024,4096]{1,0:T(8,128)(2,1)} %copy.54, bf16[]{:T(256)} %constant.116.clone.1), kind=kCustom, calls=%fused_computation.30 | custom fusion | bytes 10486272 | tf_op jit(solution)/shard_map/scatter | solution.py:86
  242.8 31.5 %while.30 = (s32[]{:T(128)}, f32[688,4096]{1,0:T(8,128)}, s32[]{:T(128)}, bf16[1280,688]{1,0:T(8,128)(2,1)}, bf16[1280,4096]{1,0:T(8,128)(2,1)}, /*index=5*/s32[]{:T(128)}, s32[]{:T(128)}, s32[]{:T(128)}, s32[]{:T(128)}) while((s32[]{:T(128)}, f32[688,4096]{1,0:T(8,128)}, s32[]{:T(128)}, bf16[1280,688]{1,0:T(8,128)(2,1)}, ...), condition=%wide.region_11.12_spmd, body=%wide.region_10.11_spmd.sunk | while | flops 724238336 | bytes 23790732 | solution.py:118
  242.8 10.5 %convolution_add_fusion.6 = f32[688,4096]{1,0:T(8,128)} fusion(f32[688,4096]{1,0:T(8,128)} %get-tuple-element.315, bf16[1280,4096]{1,0:T(8,128)(2,1)} %get-tuple-element.327, s32[]{:T(128)S(6)} %select_n.91, bf16[1280,688]{1,0:T(8,128)(2,1)} %get-tuple-element.326), kind=kOutput, calls=%fused_computation.6.clone.1 | convolution fusion | flops 724238336 | bytes 23790592 | tf_op jit(solution)/shard_map/while/body/dot_general | solution.py:111
  253.3 10.5 %convolution_add_fusion.6 = f32[688,4096]{1,0:T(8,128)} fusion(f32[688,4096]{1,0:T(8,128)} %get-tuple-element.315, bf16[1280,4096]{1,0:T(8,128)(2,1)} %get-tuple-element.327, s32[]{:T(128)S(6)} %select_n.91, bf16[1280,688]{1,0:T(8,128)(2,1)} %get-tuple-element.326), kind=kOutput, calls=%fused_computation.6.clone.1 | convolution fusion | flops 724238336 | bytes 23790592 | tf_op jit(solution)/shard_map/while/body/dot_general | solution.py:111
  263.8 10.5 %convolution_add_fusion.6 = f32[688,4096]{1,0:T(8,128)} fusion(f32[688,4096]{1,0:T(8,128)} %get-tuple-element.315, bf16[1280,4096]{1,0:T(8,128)(2,1)} %get-tuple-element.327, s32[]{:T(128)S(6)} %select_n.91, bf16[1280,688]{1,0:T(8,128)(2,1)} %get-tuple-element.326), kind=kOutput, calls=%fused_computation.6.clone.1 | convolution fusion | flops 724238336 | bytes 23790592 | tf_op jit(solution)/shard_map/while/body/dot_general | solution.py:111
  287.3 20.7 %while.31 = (s32[]{:T(128)}, f32[688,4096]{1,0:T(8,128)}, s32[]{:T(128)}, bf16[1280,688]{1,0:T(8,128)(2,1)}, bf16[1280,4096]{1,0:T(8,128)(2,1)}, /*index=5*/s32[]{:T(128)}, s32[]{:T(128)}, s32[]{:T(128)}, s32[]{:T(128)}) while((s32[]{:T(128)}, f32[688,4096]{1,0:T(8,128)}, s32[]{:T(128)}, bf16[1280,688]{1,0:T(8,128)(2,1)}, ...), condition=%wide.region_13.14_spmd, body=%wide.region_12.13_spmd.sunk | while | flops 724238336 | bytes 23790732 | solution.py:118
  287.3 10.4 %convolution_add_fusion.7 = f32[688,4096]{1,0:T(8,128)} fusion(f32[688,4096]{1,0:T(8,128)} %get-tuple-element.288, bf16[1280,4096]{1,0:T(8,128)(2,1)} %get-tuple-element.300, s32[]{:T(128)S(6)} %select_n.92, bf16[1280,688]{1,0:T(8,128)(2,1)} %get-tuple-element.299), kind=kOutput, calls=%fused_computation.10.clone.1 | convolution fusion | flops 724238336 | bytes 23790592 | tf_op jit(solution)/shard_map/while/body/dot_general | solution.py:111
  297.7 10.4 %convolution_add_fusion.7 = f32[688,4096]{1,0:T(8,128)} fusion(f32[688,4096]{1,0:T(8,128)} %get-tuple-element.288, bf16[1280,4096]{1,0:T(8,128)(2,1)} %get-tuple-element.300, s32[]{:T(128)S(6)} %select_n.92, bf16[1280,688]{1,0:T(8,128)(2,1)} %get-tuple-element.299), kind=kOutput, calls=%fused_computation.10.clone.1 | convolution fusion | flops 724238336 | bytes 23790592 | tf_op jit(solution)/shard_map/while/body/dot_general | solution.py:111
  313.7 42.0 %while.32 = (s32[]{:T(128)}, f32[688,4096]{1,0:T(8,128)}, s32[]{:T(128)}, bf16[1280,688]{1,0:T(8,128)(2,1)}, bf16[1280,4096]{1,0:T(8,128)(2,1)}, /*index=5*/s32[]{:T(128)}, s32[]{:T(128)}, s32[]{:T(128)}, s32[]{:T(128)}) while((s32[]{:T(128)}, f32[688,4096]{1,0:T(8,128)}, s32[]{:T(128)}, bf16[1280,688]{1,0:T(8,128)(2,1)}, ...), condition=%wide.region_15.16_spmd, body=%wide.region_14.15_spmd.sunk | while | flops 724238336 | bytes 23790732 | solution.py:118
  313.7 10.5 %convolution_add_fusion.8 = f32[688,4096]{1,0:T(8,128)} fusion(f32[688,4096]{1,0:T(8,128)} %get-tuple-element.261, bf16[1280,4096]{1,0:T(8,128)(2,1)} %get-tuple-element.273, s32[]{:T(128)S(6)} %select_n.93, bf16[1280,688]{1,0:T(8,128)(2,1)} %get-tuple-element.272), kind=kOutput, calls=%fused_computation.14.clone.1 | convolution fusion | flops 724238336 | bytes 23790592 | tf_op jit(solution)/shard_map/while/body/dot_general | solution.py:111
  324.2 10.6 %convolution_add_fusion.8 = f32[688,4096]{1,0:T(8,128)} fusion(f32[688,4096]{1,0:T(8,128)} %get-tuple-element.261, bf16[1280,4096]{1,0:T(8,128)(2,1)} %get-tuple-element.273, s32[]{:T(128)S(6)} %select_n.93, bf16[1280,688]{1,0:T(8,128)(2,1)} %get-tuple-element.272), kind=kOutput, calls=%fused_computation.14.clone.1 | convolution fusion | flops 724238336 | bytes 23790592 | tf_op jit(solution)/shard_map/while/body/dot_general | solution.py:111
  334.8 10.5 %convolution_add_fusion.8 = f32[688,4096]{1,0:T(8,128)} fusion(f32[688,4096]{1,0:T(8,128)} %get-tuple-element.261, bf16[1280,4096]{1,0:T(8,128)(2,1)} %get-tuple-element.273, s32[]{:T(128)S(6)} %select_n.93, bf16[1280,688]{1,0:T(8,128)(2,1)} %get-tuple-element.272), kind=kOutput, calls=%fused_computation.14.clone.1 | convolution fusion | flops 724238336 | bytes 23790592 | tf_op jit(solution)/shard_map/while/body/dot_general | solution.py:111
  345.3 10.5 %convolution_add_fusion.8 = f32[688,4096]{1,0:T(8,128)} fusion(f32[688,4096]{1,0:T(8,128)} %get-tuple-element.261, bf16[1280,4096]{1,0:T(8,128)(2,1)} %get-tuple-element.273, s32[]{:T(128)S(6)} %select_n.93, bf16[1280,688]{1,0:T(8,128)(2,1)} %get-tuple-element.272), kind=kOutput, calls=%fused_computation.14.clone.1 | convolution fusion | flops 724238336 | bytes 23790592 | tf_op jit(solution)/shard_map/while/body/dot_general | solution.py:111
  364.1 10.1 %pad_maximum_fusion = bf16[3,688,4096]{2,1,0:T(8,128)(2,1)} fusion(bf16[1,688,4096]{2,1,0:T(8,128)(2,1)S(1)} %get-tuple-element.153, bf16[1,688,4096]{2,1,0:T(8,128)(2,1)S(1)} %get-tuple-element.154, bf16[1,688,4096]{2,1,0:T(8,128)(2,1)} %convert_bitcast_fusion.2), kind=kLoop, calls=%fused_computation.26 | loop fusion | flops 16908288 | bytes 33816576 | tf_op jit(solution)/shard_map/stack | solution.py:122
  376.5 9.8 %fusion.39 = (bf16[3,688,1408]{2,1,0:T(8,128)(2,1)}, bf16[3,688,1408]{2,1,0:T(8,128)(2,1)}) fusion(bf16[3,688,4096]{2,1,0:T(8,128)(2,1)} %all-gather.5.cloned.1.call-done), kind=kLoop, calls=%fused_computation.85 | loop fusion | bytes 23248896 | tf_op jit(solution)/shard_map/jit(_take)/gather | solution.py:92
  386.2 14.1 %gather_fusion.1 = bf16[10,688,1408]{2,1,0:T(8,128)(2,1)} fusion(bf16[3,688,1408]{2,1,0:T(8,128)(2,1)} %get-tuple-element.146, s32[1024]{0:T(1024)S(1)} %pad_clamp_fusion), kind=kCustom, calls=%fused_computation.1 | custom fusion | bytes 38748200 | tf_op jit(solution)/shard_map/jit(_take)/gather | solution.py:92
  400.3 14.3 %gather_fusion.2 = bf16[10,688,1408]{2,1,0:T(8,128)(2,1)} fusion(bf16[3,688,1408]{2,1,0:T(8,128)(2,1)} %get-tuple-element.147, s32[1024]{0:T(1024)S(1)} %pad_clamp_fusion), kind=kCustom, calls=%fused_computation.2 | custom fusion | bytes 38748200 | tf_op jit(solution)/shard_map/jit(_take)/gather | solution.py:92
  419.8 10.7 %gather_fusion.3 = bf16[10,688,1280]{2,1,0:T(8,128)(2,1)} fusion(bf16[3,688,1280]{2,1,0:T(8,128)(2,1)} %mini-gather-slice.5, s32[1024]{0:T(1024)S(1)} %pad_clamp_fusion), kind=kCustom, calls=%fused_computation.3 | custom fusion | bytes 35225640 | tf_op jit(solution)/shard_map/jit(_take)/gather | solution.py:92
  430.5 99.3 %reduce-scatter.3.cloned.1.call-done = bf16[3,688,1024]{2,1,0:T(8,128)(2,1)} async-done(((bf16[3,688,4096]{2,1,0:T(8,128)(2,1)}), bf16[3,688,1024]{2,1,0:T(8,128)(2,1)}) %reduce-scatter.3.cloned.1.call-update) | async-done | bytes 4227088 | tf_op jit(solution)/shard_map/reduce_scatter | solution.py:46
  529.9 33.8 %fusion.9 = f32[10,128,688]{2,1,0:T(8,128)} fusion(bf16[10,128,4096]{2,1,0:T(8,128)(2,1)} %bitcast.34, bf16[10,688,1280]{2,1,0:T(8,128)(2,1)} %gather_fusion.3, bf16[10,688,1408]{2,1,0:T(8,128)(2,1)} %gather_fusion.2, bf16[10,688,1408]{2,1,0:T(8,128)(2,1)} %gather_fusion.1, pred[10]{0:T(512)(128)(4,1)S(1)} %compare_and_fusion), kind=kOutput, calls=%fused_computation.19 | convolution fusion | flops 7411466240 | bytes 70369288 | tf_op jit(solution)/shard_map/bkw,bfw->bkf/dot_general | solution.py:93
  (68 shorter events, 110.5 us)
Async XLA Ops:
  7.2 65.1 %all-gather.3.cloned.1.call-start = ((), (), s32[]{:S(2)}) async-start(), calls=%async_computation.6 | async-start | bytes 6340608 | tf_op jit(solution)/shard_map/all_gather | solution.py:40
  7.9 368.6 %all-gather.5.cloned.1.call-start = ((), (), s32[]{:S(2)}) async-start(), calls=%async_computation.7 | async-start | bytes 21135360 | tf_op jit(solution)/shard_map/all_gather | solution.py:40
  73.7 8.9 %all-to-all-start = ((f32[8,1,3]{2,1,0:T(1,128)}), f32[8,1,3]{2,1,0:T(1,128)S(1)}, u32[]{:S(2)}, u32[]{:S(2)}) async-start(f32[8,1,3]{2,1,0:T(1,128)} %broadcast_in_dim.15), calls=%async_computation | async-start | bytes 8192 | tf_op jit(solution)/shard_map/all_to_all | solution.py:29
  90.0 9.0 %copy-start.5 = (s32[1024]{0:T(1024)S(1)}, s32[1024]{0:T(1024)}, u32[]{:S(2)}) copy-start(s32[1024]{0:T(1024)} %param.11) | copy-start | bytes 12292
  90.0 20.4 %copy-start.4 = (bf16[1024,688]{0,1:T(8,128)(2,1)S(1)}, bf16[1024,688]{0,1:T(8,128)(2,1)}, u32[]{:S(2)}) copy-start(bf16[1024,688]{0,1:T(8,128)(2,1)} %param.13) | copy-start | bytes 4227076
  90.0 104.9 %all-to-all-start.1 = ((bf16[16,1024,256]{2,1,0:T(8,128)(2,1)}), bf16[16,1024,256]{2,1,0:T(8,128)(2,1)}, u32[]{:S(2)}, u32[]{:S(2)}) async-start(bf16[16,1024,256]{2,1,0:T(8,128)(2,1)} %stack.20), calls=%async_computation.1 | async-start | bytes 16777216 | tf_op jit(solution)/shard_map/all_to_all | solution.py:14
  99.0 430.8 %reduce-scatter.3.cloned.1.call-start = ((), (), s32[]{:S(2)}) async-start(), calls=%async_computation.4 | async-start | bytes 21135360 | tf_op jit(solution)/shard_map/reduce_scatter | solution.py:46
  111.1 96.1 %copy-start = (bf16[1024,688]{1,0:T(8,128)(2,1)}, bf16[1024,688]{1,0:T(8,128)(2,1)S(1)}, u32[]{:S(2)}) copy-start(bf16[1024,688]{1,0:T(8,128)(2,1)S(1)} %copy.50) | copy-start | bytes 4227076
  113.3 93.8 %copy-start.2 = (bf16[1024,688]{1,0:T(8,128)(2,1)}, bf16[1024,688]{1,0:T(8,128)(2,1)S(1)}, u32[]{:S(2)}) copy-start(bf16[1024,688]{1,0:T(8,128)(2,1)S(1)} %copy.51) | copy-start | bytes 4227076
  114.3 104.0 %copy-start.6 = (s32[1024,1]{0,1:T(1,128)}, s32[1024,1]{0,1:T(1,128)S(1)}, u32[]{:S(2)}) copy-start(s32[1024,1]{0,1:T(1,128)S(1)} %compare_select_fusion) | copy-start | bytes 12292
  374.1 1.7 copy-start.7
  374.2 214.9 %reduce-scatter.5.cloned.1.call-start = ((), (), s32[]{:S(2)}) async-start(), calls=%async_computation.5 | async-start | bytes 6340608 | tf_op jit(solution)/shard_map/reduce_scatter | solution.py:46
  529.9 33.8 %copy-start.8 = (s32[1024]{0:T(1024)S(1)}, s32[1024]{0:T(1024)}, u32[]{:S(2)}) copy-start(s32[1024]{0:T(1024)} %broadcast_clamp_fusion) | copy-start | bytes 12292
  563.7 8.1 %copy-start.1 = (bf16[1024,688]{1,0:T(8,128)(2,1)S(1)}, bf16[1024,688]{1,0:T(8,128)(2,1)}, u32[]{:S(2)}) copy-start(bf16[1024,688]{1,0:T(8,128)(2,1)} %copy-done) | copy-start | bytes 4227076
  563.7 8.1 %copy-start.3 = (bf16[1024,688]{1,0:T(8,128)(2,1)S(1)}, bf16[1024,688]{1,0:T(8,128)(2,1)}, u32[]{:S(2)}) copy-start(bf16[1024,688]{1,0:T(8,128)(2,1)} %copy-done.2) | copy-start | bytes 4227076
Sparse Core Ops, SparseCore 0:
  9.6 62.6 all-gather.2
  74.0 157.2 all-gather.4
  374.3 155.5 reduce-scatter.2
  532.1 56.9 reduce-scatter.4
